TPU v7x, 256 devices: a 8x8x2 block of a 8x8x16 slice. The times are simulated.
256 devices in a mesh: ga: 2 (over z), aa: 64 (over y, x), ba: 2 (over core).
Axes of the slice: x: 8, y: 8, z: 2, core: 2. Of those that a mesh axis runs over, the one named last changes fastest.
The devices are a block of a 8x8x16 slice.
Arguments:
- images: bfloat16 [16384, 12, 4096], P(('ga', 'aa', 'ba')), parts along dimension 0, may hold values from -6 to 6
- key_projection: bfloat16 [4096, 512], replicated, may hold values from -0.09375 to 0.09375
- value_projection: bfloat16 [4096, 512], replicated, may hold values from -0.09375 to 0.09375
- key_norm_gain: float32 [128], replicated, may hold values from 0.1 to 1.9
- hidden: bfloat16 [16384, 4096], P(('ga', 'aa'), 'ba'), parts along dimension 0, may hold values from -6 to 6
- shared_query_base: bfloat16 [16384, 2048], P(('ga', 'aa'), 'ba'), parts along dimension 0, may hold values from -220 to 220
- adapter_down_matrix: bfloat16 [64, 4096, 16], P('aa'), may hold values from -0.09375 to 0.09375
- adapter_up_matrix: bfloat16 [64, 16, 2048], P('aa'), may hold values from -1.5 to 1.5
- tenant_adapter_index: int32 [16384, 1], P(('ga', 'aa')), parts along dimension 0, may hold values from 0 to 63; in each aligned block of 128 rows (0 to 127, 128 to 255, ...) at most 4 rows name the same one
- used_tile_count: int32 [16384], P(('ga', 'aa', 'ba')), parts along dimension 0, may hold values from 1 to 4
Outputs:
- attended: bfloat16 [16384, 2048], P(('ga', 'aa', 'ba')), parts along dimension 0
There are 2 independent parts, one for each index of `ga`. A program takes and returns all parts, laid end to end along the dimension named above; an argument that names none is the same for every part. Nothing has to cross between parts.
Inputs may be any that keep to these rules, and one draw needn't show every extreme that they name: `tenant_adapter_index`: among the 128 requests of one index of aa (aligned blocks) no adapter is named more than 4 times.
All inputs are finite; a program needn't handle non-finite values.
Results may differ from a plain program's by a relative error of at most 0.012.
The roundings to bfloat16 on the way count: a program that leaves them out, or rounds other values in their place, can miss the bound.
Values may be sent and summed in bfloat16 or wider, within the bound.
A program may use at most 128 MiB of HBM per device.

v0:
```python
import math

import jax
import jax.numpy as jnp
from jax import lax
from jax.sharding import PartitionSpec as P

TILE_TOKENS = 3


def copy_for_each(value, axis):
    peers = lax.axis_size(axis)
    return lax.all_to_all(
        jnp.broadcast_to(value[None], (peers, *value.shape)), axis, 0, 0, tiled=True
    )


def taken_together(value, axis):
    return copy_for_each(value, axis).sum(axis=0)


def on_device(
    images,
    key_projection,
    value_projection,
    key_norm_gain,
    hidden,
    shared_query_base,
    adapter_down_matrix,
    adapter_up_matrix,
    tenant_adapter_index,
    used_tile_count,
):
    requests = hidden.shape[0]
    half_model = hidden.shape[1]
    half_query = shared_query_base.shape[1]
    head_size = key_norm_gain.shape[0]
    heads_kv = key_projection.shape[1] // head_size
    bank_count = lax.axis_size("aa")
    slots_most = 2 * requests // bank_count
    our_side = lax.axis_index("ba")
    owner_ids = tenant_adapter_index[:, 0]
    owner_hot = (owner_ids[:, None] == jnp.arange(bank_count, dtype=jnp.int32)[None, :]).astype(
        jnp.float32
    )
    lower_ones = (jnp.arange(requests)[:, None] > jnp.arange(requests)[None, :]).astype(
        jnp.bfloat16
    )
    before = jnp.dot(lower_ones, owner_hot.astype(jnp.bfloat16), preferred_element_type=jnp.float32)
    rank_in = jnp.sum(before * owner_hot, axis=1)
    slot_hot = (rank_in[:, None] == jnp.arange(slots_most, dtype=jnp.float32)[None, :]).astype(
        jnp.float32
    )
    placing = (
        (owner_hot[:, :, None] * slot_hot[:, None, :])
        .reshape(requests, bank_count * slots_most)
        .astype(jnp.bfloat16)
    )
    down_half = lax.dynamic_slice_in_dim(
        adapter_down_matrix[0], our_side * half_model, half_model, 0
    )
    up_half = lax.dynamic_slice_in_dim(adapter_up_matrix[0], our_side * half_query, half_query, 1)
    packed = lax.dot_general(
        placing, hidden, (((0,), (0,)), ((), ())), preferred_element_type=jnp.float32
    )
    received_rows = lax.all_to_all(
        packed.astype(jnp.bfloat16).reshape(bank_count, slots_most, hidden.shape[1]),
        "aa",
        split_axis=0,
        concat_axis=0,
        tiled=True,
    )
    low_part = jnp.dot(
        received_rows.reshape(-1, half_model), down_half, preferred_element_type=jnp.float32
    )
    reduced_rank_part = taken_together(low_part, "ba")
    raised_output = jnp.dot(
        reduced_rank_part.astype(jnp.bfloat16), up_half, preferred_element_type=jnp.float32
    )
    raised_output = raised_output.astype(jnp.bfloat16).reshape(
        received_rows.shape[0], received_rows.shape[1], half_query
    )
    returned = lax.all_to_all(raised_output, "aa", split_axis=0, concat_axis=0, tiled=True)
    flat_back = returned.reshape(bank_count * slots_most, returned.shape[2])
    delta_half = jnp.dot(placing, flat_back, preferred_element_type=jnp.float32)
    query_half = (shared_query_base.astype(jnp.float32) + delta_half).astype(jnp.bfloat16)
    query_rows = lax.all_to_all(query_half, "ba", split_axis=0, concat_axis=1, tiled=True)
    requests_here = images.shape[0]
    local_rows = images.shape[1]
    flattened_rows = images.reshape(requests_here * local_rows, images.shape[2])
    unnormed_keys = jnp.dot(
        flattened_rows, key_projection, preferred_element_type=jnp.float32
    ).reshape(requests_here, local_rows, heads_kv, head_size)
    key_scale = lax.rsqrt(jnp.mean(unnormed_keys * unnormed_keys, axis=-1, keepdims=True) + 1e-06)
    keys_local = (unnormed_keys * key_scale * key_norm_gain).astype(jnp.bfloat16)
    values_local = jnp.dot(
        flattened_rows, value_projection, preferred_element_type=jnp.float32
    ).astype(jnp.bfloat16)
    values_local = values_local.reshape(requests_here, local_rows, heads_kv, head_size)
    query_group_width = query_rows.shape[1] // (heads_kv * head_size)
    query_four_axes = query_rows.reshape(requests_here, heads_kv, query_group_width, head_size)
    scores = jnp.einsum(
        "rkgd,rjkd->rkgj", query_four_axes, keys_local, preferred_element_type=jnp.float32
    ) / math.sqrt(head_size)
    position = jnp.arange(local_rows, dtype=jnp.int32) // TILE_TOKENS
    valid_rows = position[None, :] < used_tile_count[:, None]
    key_mask = valid_rows[:, None, None, :]
    masked = jnp.where(key_mask, scores, -1e30)
    score_peak = jnp.max(masked, axis=-1)
    weights = jnp.where(key_mask, jnp.exp(masked - score_peak[..., None]), 0.0)
    weight_total = jnp.sum(weights, axis=-1)
    weighted = jnp.einsum(
        "rkgj,rjkd->rkgd",
        weights.astype(jnp.bfloat16),
        values_local,
        preferred_element_type=jnp.float32,
    )
    attended = (weighted / weight_total[..., None]).reshape(requests_here, -1).astype(jnp.bfloat16)
    return attended


def solution(mesh):
    placed = (
        P(("ga", "aa", "ba"), None, None),
        P(),
        P(),
        P(),
        P(("ga", "aa"), "ba"),
        P(("ga", "aa"), "ba"),
        P("aa", None, None),
        P("aa", None, None),
        P(("ga", "aa"), None),
        P(("ga", "aa", "ba")),
    )
    return jax.shard_map(
        on_device,
        mesh=mesh,
        in_specs=placed,
        out_specs=P(("ga", "aa", "ba"), None),
        check_vma=False,
    )
```

profile of v0, /device:TPU:513, one launch (start us, length us, event | category | flops | bytes accessed | tf_op | source)
XLA Modules:
  0.0 111.0 jit_solution(15379478204448119320)
XLA Ops:
  0.0 0.0 copy-start
  0.0 0.9 fusion.10
  0.9 0.7 fusion.21
  1.6 0.0 copy-done
  1.6 0.4 convolution_convert_fusion
  2.1 1.2 %reshape.126 = bf16[64,4,2048]{2,1,0:T(4,128)(2,1)} reshape(bf16[256,2048]{1,0:T(8,128)(2,1)S(1)} %convolution_convert_fusion) | data formatting | bytes 2097152 | tf_op jit(solution)/shard_map/reshape | solution.py:67
  3.3 21.8 %all-to-all-start = ((bf16[64,4,2048]{2,1,0:T(4,128)(2,1)}), bf16[64,4,2048]{2,1,0:T(4,128)(2,1)S(1)}, u32[]{:S(2)}, u32[]{:S(2)}) async-start(bf16[64,4,2048]{2,1,0:T(4,128)(2,1)} %reshape.126), calls=%async_computation | async-start | bytes 2097152 | tf_op jit(solution)/shard_map/all_to_all | solution.py:66
  25.1 9.6 %copy.35 = bf16[64,12,4096]{2,1,0:T(8,128)(2,1)} copy(bf16[64,12,4096]{2,0,1:T(8,128)(2,1)} %param.10) | data formatting | bytes 12582912 | tf_op args[0]
  34.7 9.9 %reshape.130 = bf16[768,4096]{1,0:T(8,128)(2,1)} reshape(bf16[64,12,4096]{2,1,0:T(8,128)(2,1)} %copy.35) | data formatting | bytes 12582912 | tf_op jit(solution)/shard_map/reshape | solution.py:90
  44.6 6.4 %copy.38 = bf16[512,4096]{1,0:T(8,128)(2,1)} copy(bf16[512,4096]{0,1:T(8,128)(2,1)} %bitcast.36) | data formatting | bytes 8388608 | tf_op jit(solution)/shard_map/dot_general | solution.py:91
  51.0 0.0 copy-start.2
  51.0 0.0 copy-start.3
  51.0 7.9 %multiply_reduce_fusion = (f32[64,12,4]{0,2,1:T(4,128)S(1)}, f32[64,12,4,128]{3,0,2,1:T(8,128)}) fusion(bf16[4,128,4096,1]{2,1,0,3:T(8,128)(2,1)} %bitcast.37, bf16[64,12,4096]{2,0,1:T(8,128)(2,1)} %param.10), kind=kOutput, calls=%fused_computation.5 | convolution fusion | flops 3222008832 | bytes 12070912 | tf_op jit(solution)/shard_map/dot_general | solution.py:91
  58.9 0.0 all-to-all-done
  58.9 0.3 reshape.127
  59.2 0.0 copy-done.2
  59.2 0.4 fusion.15
  59.6 8.5 %all_to_all.31 = f32[2,256,16]{1,2,0:T(8,128)S(1)} all-to-all(f32[2,256,16]{1,2,0:T(8,128)S(1)} %broadcast_in_dim.17), channel_id=1, replica_groups=mesh['ga'=2,'aa'=64,'ba'=2] {'ba'}, dimensions={0} | all-to-all | bytes 65536 | tf_op jit(solution)/shard_map/all_to_all | solution.py:13
  68.1 0.0 copy-done.3
  68.1 0.3 convolution_convert_fusion.2
  68.5 1.0 reshape.128
  69.5 13.6 %all-to-all-start.2 = ((bf16[64,4,1024]{2,1,0:T(4,128)(2,1)}), bf16[64,4,1024]{2,1,0:T(4,128)(2,1)S(1)}, u32[]{:S(2)}, u32[]{:S(2)}) async-start(bf16[64,4,1024]{2,1,0:T(4,128)(2,1)} %reshape.128), calls=%async_computation.2 | async-start | bytes 1048576 | tf_op jit(solution)/shard_map/all_to_all | solution.py:83
  83.1 0.0 copy-start.4
  83.1 0.0 copy-start.1
  83.1 0.0 copy-start.5
  83.1 8.4 %convolution_convert_fusion.1 = bf16[768,512]{1,0:T(8,128)(2,1)} fusion(bf16[768,4096]{1,0:T(8,128)(2,1)} %reshape.130, bf16[4096,512]{1,0:T(8,128)(2,1)} %param.12), kind=kOutput, calls=%fused_computation.6 | convolution fusion | flops 3221618688 | bytes 11272192 | tf_op jit(solution)/shard_map/dot_general | solution.py:96
  91.5 1.7 %reshape.131 = bf16[64,12,4,128]{3,2,1,0:T(4,128)(2,1)S(1)} reshape(bf16[768,512]{1,0:T(8,128)(2,1)} %convolution_convert_fusion.1) | data formatting | bytes 1572864 | tf_op jit(solution)/shard_map/reshape | solution.py:99
  93.3 0.0 copy-done.4
  93.3 0.1 broadcast_compare_fusion
  93.4 0.0 copy-done.1
  93.4 0.0 copy-done.5
  93.4 1.4 %multiply_convert_fusion = bf16[64,12,4,128]{3,0,2,1:T(8,128)(2,1)} fusion(f32[64,12,4,128]{3,0,2,1:T(8,128)S(1)} %copy-done.1, f32[128]{0:T(128)S(1)} %copy-done.5, f32[64,12,4]{0,2,1:T(4,128)S(1)} %add_rsqrt_fusion), kind=kLoop, calls=%fused_computation.4 | loop fusion | flops 1179648 | bytes 2372096 | tf_op jit(solution)/shard_map/convert_element_type | solution.py:95
  94.8 4.4 %all-to-all-done.2 = bf16[64,4,1024]{2,1,0:T(4,128)(2,1)S(1)} async-done(((bf16[64,4,1024]{2,1,0:T(4,128)(2,1)}), bf16[64,4,1024]{2,1,0:T(4,128)(2,1)S(1)}, u32[]{:S(2)}, u32[]{:S(2)}) %all-to-all-start.2) | async-done | bytes 524320 | tf_op jit(solution)/shard_map/all_to_all | solution.py:83
  99.2 1.3 %fusion.9 = bf16[128,1024]{1,0:T(8,128)(2,1)S(1)} fusion(bf16[64,4,1024]{2,1,0:T(4,128)(2,1)S(1)} %all-to-all-done.2, bf16[128,1024]{1,0:T(8,128)(2,1)} %param.15, bf16[128,64,4]{0,2,1:T(4,128)(2,1)S(1)} %multiply_convert_fusion.1), kind=kOutput, calls=%fused_computation.17 | convolution fusion | flops 67502080 | bytes 1114112 | tf_op jit(solution)/shard_map/dot_general | solution.py:85
  100.5 6.4 %all_to_all.32 = bf16[2,64,1024]{2,1,0:T(8,128)(2,1)S(1)} all-to-all(bf16[2,64,1024]{2,1,0:T(8,128)(2,1)S(1)} %bitcast.38), channel_id=1, replica_groups=mesh['ga'=2,'aa'=64,'ba'=2] {'ba'}, dimensions={0} | all-to-all | bytes 524288 | tf_op jit(solution)/shard_map/all_to_all | solution.py:87
  106.8 0.3 copy.32
  107.1 0.2 reshape.129
  107.3 2.3 %fusion.28 = (f32[64,4,4]{2,1,0:T(4,128)S(1)}, bf16[64,4,4,12]{3,2,1,0:T(4,128)(2,1)S(1)}) fusion(pred[64,12]{1,0:T(8,128)(4,1)S(1)} %broadcast_compare_fusion, bf16[64,4,4,128]{3,2,1,0:T(4,128)(2,1)S(1)} %reshape.129, bf16[64,12,4,128]{3,0,2,1:T(8,128)(2,1)} %multiply_convert_fusion), kind=kOutput, calls=%fused_computation.46 | convolution fusion | flops 3219467 | bytes 1078016 | tf_op jit(solution)/shard_map/sub | solution.py:110
  109.6 0.5 fusion.8
  110.1 0.9 convert_element_type.69
  (6 shorter events, 0.1 us)
Async XLA Ops:
  0.0 1.6 %copy-start = (bf16[128,2048]{1,0:T(8,128)(2,1)S(1)}, bf16[128,2048]{1,0:T(8,128)(2,1)}, u32[]{:S(2)}) copy-start(bf16[128,2048]{1,0:T(8,128)(2,1)} %param.14) | copy-start | bytes 1572868
  3.3 55.6 %all-to-all-start = ((bf16[64,4,2048]{2,1,0:T(4,128)(2,1)}), bf16[64,4,2048]{2,1,0:T(4,128)(2,1)S(1)}, u32[]{:S(2)}, u32[]{:S(2)}) async-start(bf16[64,4,2048]{2,1,0:T(4,128)(2,1)} %reshape.126), calls=%async_computation | async-start | bytes 2097152 | tf_op jit(solution)/shard_map/all_to_all | solution.py:66
  51.0 8.2 %copy-start.2 = (bf16[1,4096,16]{1,2,0:T(8,128)(2,1)S(1)}, bf16[1,4096,16]{1,2,0:T(8,128)(2,1)}, u32[]{:S(2)}) copy-start(bf16[1,4096,16]{1,2,0:T(8,128)(2,1)} %param.16) | copy-start | bytes 393220
  51.0 17.2 %copy-start.3 = (bf16[1,16,2048]{2,1,0:T(8,128)(2,1)S(1)}, bf16[1,16,2048]{2,1,0:T(8,128)(2,1)}, u32[]{:S(2)}) copy-start(bf16[1,16,2048]{2,1,0:T(8,128)(2,1)} %param.17) | copy-start | bytes 196612
  69.5 29.7 %all-to-all-start.2 = ((bf16[64,4,1024]{2,1,0:T(4,128)(2,1)}), bf16[64,4,1024]{2,1,0:T(4,128)(2,1)S(1)}, u32[]{:S(2)}, u32[]{:S(2)}) async-start(bf16[64,4,1024]{2,1,0:T(4,128)(2,1)} %reshape.128), calls=%async_computation.2 | async-start | bytes 1048576 | tf_op jit(solution)/shard_map/all_to_all | solution.py:83
  83.1 10.2 %copy-start.4 = (s32[64]{0:T(128)S(1)}, s32[64]{0:T(128)}, u32[]{:S(2)}) copy-start(s32[64]{0:T(128)} %param.19) | copy-start | bytes 772
  83.1 10.3 %copy-start.1 = (f32[64,12,4,128]{3,0,2,1:T(8,128)S(1)}, f32[64,12,4,128]{3,0,2,1:T(8,128)}, u32[]{:S(2)}) copy-start(f32[64,12,4,128]{3,0,2,1:T(8,128)} %get-tuple-element.6) | copy-start | bytes 4718596
  83.1 10.3 %copy-start.5 = (f32[128]{0:T(128)S(1)}, f32[128]{0:T(128)}, u32[]{:S(2)}) copy-start(f32[128]{0:T(128)} %param.13) | copy-start | bytes 1540
where the time goes:
time: 112 us; the launch traced here: 111 us
  starting transfers between devices  35.4 us (32%)
  local copies, waits for them, and re-layouts  31.5 us (28%)
  matrix products  22.4 us (20%)
  blocking collectives  14.9 us (13%)
  waiting for transfers between devices  4.39 us (4%)
  other arithmetic  2.17 us (2%)
    all_to_all x1, starting transfers between devices, on_device(): lax.all_to_all(packed.astype(jnp.bfloat16).reshape(bank_count, slots_most...  21.8 us
    all_to_all x1, starting transfers between devices, on_device(): lax.all_to_all(raised_output, 'aa', split_axis=0, concat_axis=0, tiled=True)  13.6 us
    reshape x1, local copies, waits for them, and re-layouts, on_device(): flattened_rows = images.reshape(requests_here * local_rows, images.shape[2])  9.85 us
    unnamed x13, local copies, waits for them, and re-layouts  9.64 us
    all_to_all x1, blocking collectives, copy_for_each(): lax.all_to_all(jnp.broadcast_to(value[None], (peers, *value.shape)), axis...  8.54 us
    dot_general x1, matrix products, on_device(): jnp.dot(flattened_rows, value_projection, preferred_element_type=jnp.floa...  8.41 us
    dot_general x1, matrix products, on_device(): jnp.dot(flattened_rows, key_projection, preferred_element_type=jnp.float32)  7.94 us
    dot_general x1, local copies, waits for them, and re-layouts, on_device(): jnp.dot(flattened_rows, key_projection, preferred_element_type=jnp.float32)  6.41 us
  transfers between devices with their start and end apart: 2, of which 1 were waited for; matrix products, arithmetic and copies ran while one was open for 41% of the time, Pallas kernels for 0%

commit v1 on v0

v1 whole, which is shorter than its diff:
```python
import functools
import math

import jax
import jax.numpy as jnp
from jax import lax
from jax.experimental import pallas as pl
from jax.experimental.pallas import tpu as pltpu
from jax.sharding import PartitionSpec as P

TILE_TOKENS = 3
BLOCK = 16
MESH = pl.DeviceIdType.MESH
F32 = jnp.float32
BF16 = jnp.bfloat16
NT = (((1,), (1,)), ((), ()))
TN = (((0,), (0,)), ((), ()))


def dot(a, b, dims=(((1,), (0,)), ((), ()))):
    return lax.dot_general(a, b, dims, preferred_element_type=F32)


def iota(shape, dim):
    return lax.broadcasted_iota(jnp.int32, shape, dim)


def kernel(
    side,
    most,
    images,
    wk,
    wv,
    gain,
    hidden,
    base,
    down,
    up,
    ids,
    used,
    out,
    images_v,
    wk_v,
    wv_v,
    gain_v,
    hidden_v,
    base_v,
    ids_v,
    used_v,
    adapters,
    packed,
    placing,
    received,
    low_own,
    low_other,
    raised,
    returned,
    q_own,
    q_send,
    q_other,
    keys,
    values,
    bias,
    local_sem,
    adapter_send,
    adapter_recv,
    row_send,
    row_recv,
    back_send,
    back_recv,
    low_send,
    low_recv,
    q_send_sem,
    q_recv_sem,
):
    me = lax.axis_index("aa")
    core = lax.axis_index("ba")
    y, x = me // side, me % side
    partner = {"ba": 1 - core}
    parity = (y + x) % 2
    banks = side * side
    group = side // 2
    chunk = group * most
    requests, half_model = hidden.shape
    half_query = base.shape[1]
    rank = up.shape[0]
    tokens, ours = keys.shape[0], keys.shape[1]
    head = gain.shape[1]

    def down_column(k):
        return {"aa": ((y + k) % side) * side + x}

    def along_row(k):
        return {"aa": y * side + (x + k) % side}

    own_slot = parity * (group + y // 2) + (1 - parity) * (x // 2)

    barrier = pltpu.get_barrier_semaphore()
    pl.semaphore_signal(barrier, inc=1, device_id=partner, device_id_type=MESH)
    for k in range(1, side):
        pl.semaphore_signal(barrier, inc=1, device_id=down_column(k), device_id_type=MESH)
        pl.semaphore_signal(barrier, inc=1, device_id=along_row(k), device_id_type=MESH)

    model_at = pl.multiple_of(core * half_model, half_model)
    query_at = pl.multiple_of(core * half_query, half_query)
    own_down = adapters.at[own_slot, :, pl.ds(0, half_model)]
    own_up = adapters.at[own_slot, :, pl.ds(half_model, half_query)]
    pairs = (
        (ids, ids_v),
        (hidden, hidden_v),
        (down.at[:, pl.ds(model_at, half_model)], own_down),
        (up.at[:, pl.ds(query_at, half_query)], own_up),
        (used, used_v),
        (gain, gain_v),
        (images, images_v),
        (wk, wk_v),
        (wv, wv_v),
        (base, base_v),
    )
    local = [pltpu.make_async_copy(s, d, local_sem.at[i]) for i, (s, d) in enumerate(pairs)]
    for copy in local:
        copy.start()

    local[0].wait()
    owner = ids_v[...]
    hot = (iota((banks, requests), 0) == owner).astype(BF16)
    earlier = (iota((requests, requests), 0) < iota((requests, requests), 1)).astype(BF16)
    before = dot(hot, earlier)
    standing = jnp.sum(before * hot.astype(F32), axis=0, keepdims=True).astype(jnp.int32)
    shift = side.bit_length() - 1
    owner_y, owner_x = owner >> shift, owner & (side - 1)
    odd = (owner_y + owner_x) & 1
    place = jnp.where(
        odd == 0,
        owner_y * group + (owner_x >> 1),
        banks // 2 + owner_x * group + (owner_y >> 1),
    )
    slot = place * most + standing
    placing[...] = (iota((banks * most, requests), 0) == slot).astype(BF16)
    local[1].wait()
    packed[...] = (
        dot(placing[...], hidden_v[...]).astype(BF16).reshape(2 * side, chunk, half_model)
    )
    received[y] = packed[y]
    received[side + x] = packed[side + x]
    local[2].wait()
    local[3].wait()

    pl.semaphore_wait(barrier, 2 * side - 1)

    sends = []

    def send(source, target, send_sem, recv_sem, device):
        copy = pltpu.make_async_remote_copy(
            src_ref=source,
            dst_ref=target,
            send_sem=send_sem,
            recv_sem=recv_sem,
            device_id=device,
            device_id_type=MESH,
        )
        copy.start()
        sends.append(copy)
        return copy

    order = sorted(range(1, side), key=lambda k: -min(k, side - k))
    for k in order:
        peer = parity * ((y + k) % side * side + x) + (1 - parity) * (y * side + (x + k) % side)
        send(
            adapters.at[own_slot],
            adapters.at[own_slot],
            adapter_send.at[k],
            adapter_recv.at[own_slot],
            {"aa": peer},
        )
    for k in order:
        to_y, to_x = (y + k) % side, (x + k) % side
        send(packed.at[to_y], received.at[y], row_send.at[k], row_recv.at[y], down_column(k))
        send(
            packed.at[side + to_x],
            received.at[side + x],
            row_send.at[side + k],
            row_recv.at[side + x],
            along_row(k),
        )

    local[4].wait()
    local[5].wait()
    local[6].wait()
    local[7].wait()
    wide = 2 * head

    def project_keys(n, carry):
        at = pl.multiple_of(n * wide, wide)
        raw = dot(images_v[...], wk_v[:, pl.ds(at, wide)])
        for part in range(2):
            one = raw[:, part * head : (part + 1) * head]
            scale = lax.rsqrt(jnp.mean(one * one, axis=1, keepdims=True) + 1e-06)
            keys[:, :, pl.ds(pl.multiple_of(at + part * head, head), head)] = (
                (one * scale * gain_v[...]).astype(BF16).reshape(tokens, ours, head)
            )
        return carry

    lax.fori_loop(0, wk.shape[1] // wide, project_keys, 0)
    local[8].wait()

    def project_values(n, carry):
        at = pl.multiple_of(n * wide, wide)
        raw = dot(images_v[...], wv_v[:, pl.ds(at, wide)])
        values[:, :, pl.ds(at, wide)] = raw.astype(BF16).reshape(tokens, ours, wide)
        return carry

    lax.fori_loop(0, wv.shape[1] // wide, project_values, 0)

    lanes = tokens * BLOCK
    heads_each = (2 * half_query // head) // (wk.shape[1] // head)
    rows = heads_each * BLOCK
    token = iota((1, lanes), 1) // BLOCK
    tile = jnp.zeros((1, lanes), jnp.int32)
    for edge in range(TILE_TOKENS, tokens, TILE_TOKENS):
        tile = tile + (token >= edge).astype(jnp.int32)
    counts = jnp.broadcast_to(used_v[...].astype(F32), (8, ours)).astype(BF16)
    same = (iota((rows, lanes), 0) & (BLOCK - 1)) == (iota((rows, lanes), 1) & (BLOCK - 1))
    for b in range(ours // BLOCK):
        spread = (
            iota((ours, lanes), 0) == b * BLOCK + (iota((ours, lanes), 1) & (BLOCK - 1))
        ).astype(BF16)
        count = dot(counts, spread)[0:1]
        bias[b] = jnp.where(same & (tile.astype(F32) < count), 0.0, -1e30)

    def arrived(ref, send_sem, recv_sem):
        pltpu.make_async_remote_copy(
            src_ref=ref,
            dst_ref=ref,
            send_sem=send_sem,
            recv_sem=recv_sem,
            device_id=partner,
            device_id_type=MESH,
        ).wait_recv()

    for k in range(1, side):
        other = (own_slot + k) % side
        arrived(adapters.at[other], adapter_send.at[k], adapter_recv.at[other])
    slots = side * chunk
    in_slot = (iota((slots, group * rank), 0) & (chunk - 1)) // most
    keep = in_slot == iota((slots, group * rank), 1) // rank
    for kind, here in ((0, y), (1, x)):
        for k in range(1, side):
            source = kind * side + (here + k) % side
            arrived(received.at[source], row_send.at[k], row_recv.at[source])
        low = dot(
            received[kind * side : (kind + 1) * side].reshape(slots, half_model),
            adapters[kind * group : (kind + 1) * group, :, :half_model].reshape(
                group * rank, half_model
            ),
            NT,
        )
        low_own[kind] = jnp.where(keep, low, 0.0)
    send(low_own, low_other, low_send, low_recv, partner)
    arrived(low_other, low_send, low_recv)
    for kind in range(2):
        low = (low_own[kind] + low_other[kind]).astype(BF16)
        result = dot(
            low,
            adapters[kind * group : (kind + 1) * group, :, half_model:].reshape(
                group * rank, half_query
            ),
        )
        raised[kind * side : (kind + 1) * side] = result.astype(BF16).reshape(
            side, chunk, half_query
        )
    returned[y] = raised[y]
    returned[side + x] = raised[side + x]
    for k in order:
        to_y, to_x = (y + k) % side, (x + k) % side
        send(raised.at[to_y], returned.at[y], back_send.at[k], back_recv.at[y], down_column(k))
        send(
            raised.at[side + to_x],
            returned.at[side + x],
            back_send.at[side + k],
            back_recv.at[side + x],
            along_row(k),
        )
    local[9].wait()
    for kind, here in ((0, y), (1, x)):
        for k in range(1, side):
            source = kind * side + (here + k) % side
            arrived(returned.at[source], back_send.at[k], back_recv.at[source])
    delta = dot(placing[...], returned[...].reshape(banks * most, half_query), TN)
    query = (base_v[...].astype(F32) + delta).astype(BF16)
    q_own[...] = query.reshape(2, ours, half_query)
    q_send[...] = q_own[1 - core]
    send(q_send, q_other, q_send_sem, q_recv_sem, partner)

    def attend(q, part):
        for b in range(ours // BLOCK):
            at = slice(b * BLOCK, (b + 1) * BLOCK)
            for g in range(half_query // head // heads_each):
                first = part * half_query + g * heads_each * head
                kv = pl.multiple_of(
                    part * (half_query // heads_each) + g * head, head
                )
                block = jnp.concatenate(
                    [
                        q[at, (g * heads_each + i) * head : (g * heads_each + i + 1) * head]
                        for i in range(heads_each)
                    ],
                    axis=0,
                )
                key = keys[:, at, pl.ds(kv, head)].reshape(lanes, head)
                value = values[:, at, pl.ds(kv, head)].reshape(lanes, head)
                score = dot(block, key, NT) * (1.0 / math.sqrt(head)) + bias[b]
                weight = jnp.exp(score - jnp.max(score, axis=1, keepdims=True))
                total = jnp.sum(weight, axis=1, keepdims=True)
                result = (dot(weight.astype(BF16), value) / total).astype(BF16)
                for i in range(heads_each):
                    out[at, pl.ds(pl.multiple_of(first + i * head, head), head)] = result[
                        i * BLOCK : (i + 1) * BLOCK
                    ]

    attend(q_own[core], core)
    arrived(q_other, q_send_sem, q_recv_sem)
    attend(q_other[...], 1 - core)
    for copy in sends:
        copy.wait_send()


def on_device(
    side,
    images,
    key_projection,
    value_projection,
    key_norm_gain,
    hidden,
    shared_query_base,
    adapter_down_matrix,
    adapter_up_matrix,
    tenant_adapter_index,
    used_tile_count,
):
    ours, tokens, model = images.shape
    requests, half_model = hidden.shape
    half_query = shared_query_base.shape[1]
    head = key_norm_gain.shape[0]
    kvw = key_projection.shape[1]
    banks = side * side
    most = 2 * requests // banks
    group = side // 2
    chunk = group * most
    rank = adapter_up_matrix.shape[1]
    heads_each = 2 * half_query // kvw
    args = (
        jnp.transpose(images, (1, 0, 2)).reshape(tokens * ours, model),
        key_projection,
        value_projection,
        key_norm_gain.reshape(1, head),
        hidden,
        shared_query_base,
        jnp.transpose(adapter_down_matrix[0]),
        adapter_up_matrix[0],
        tenant_adapter_index.reshape(1, requests),
        used_tile_count.reshape(1, ours),
    )
    dma = pltpu.SemaphoreType.DMA
    return pl.pallas_call(
        functools.partial(kernel, side, most),
        out_shape=jax.ShapeDtypeStruct((ours, 2 * half_query), BF16),
        in_specs=[pl.BlockSpec(memory_space=pl.ANY)] * len(args),
        out_specs=pl.BlockSpec(memory_space=pltpu.VMEM),
        scratch_shapes=[
            pltpu.VMEM((tokens * ours, model), BF16),
            pltpu.VMEM((model, kvw), BF16),
            pltpu.VMEM((model, kvw), BF16),
            pltpu.VMEM((1, head), F32),
            pltpu.VMEM((requests, half_model), BF16),
            pltpu.VMEM((requests, half_query), BF16),
            pltpu.VMEM((1, requests), jnp.int32),
            pltpu.VMEM((1, ours), jnp.int32),
            pltpu.VMEM((side, rank, half_model + half_query), BF16),
            pltpu.VMEM((2 * side, chunk, half_model), BF16),
            pltpu.VMEM((banks * most, requests), BF16),
            pltpu.VMEM((2 * side, chunk, half_model), BF16),
            pltpu.VMEM((2, side * chunk, group * rank), F32),
            pltpu.VMEM((2, side * chunk, group * rank), F32),
            pltpu.VMEM((2 * side, chunk, half_query), BF16),
            pltpu.VMEM((2 * side, chunk, half_query), BF16),
            pltpu.VMEM((2, ours, half_query), BF16),
            pltpu.VMEM((ours, half_query), BF16),
            pltpu.VMEM((ours, half_query), BF16),
            pltpu.VMEM((tokens, ours, kvw), BF16),
            pltpu.VMEM((tokens, ours, kvw), BF16),
            pltpu.VMEM((ours // BLOCK, heads_each * BLOCK, tokens * BLOCK), F32),
            dma((10,)),
            dma((side,)),
            dma((side,)),
            dma((2 * side,)),
            dma((2 * side,)),
            dma((2 * side,)),
            dma((2 * side,)),
            dma(()),
            dma(()),
            dma(()),
            dma(()),
        ],
        compiler_params=pltpu.CompilerParams(collective_id=0, has_side_effects=True),
        name="adapter_attention",
    )(*args)


def solution(mesh):
    placed = (
        P(("ga", "aa", "ba"), None, None),
        P(),
        P(),
        P(),
        P(("ga", "aa"), "ba"),
        P(("ga", "aa"), "ba"),
        P("aa", None, None),
        P("aa", None, None),
        P(("ga", "aa"), None),
        P(("ga", "aa", "ba")),
    )
    return jax.shard_map(
        functools.partial(on_device, math.isqrt(mesh.shape["aa"])),
        mesh=mesh,
        in_specs=placed,
        out_specs=P(("ga", "aa", "ba"), None),
        check_vma=False,
    )
```

time: 112 us -> 60.1 us (0.54)
  Pallas kernels: 0 us -> 58.3 us
  starting transfers between devices: 35.4 us -> 0 us
  local copies, waits for them, and re-layouts: 31.5 us -> 1.67 us
  matrix products: 22.4 us -> 0 us
  blocking collectives: 14.9 us -> 0 us
  waiting for transfers between devices: 4.39 us -> 0 us
  other arithmetic: 2.17 us -> 0 us
    pallas_call x0 -> x1, Pallas kernels: none -> 58.3 us  [on_device(): pl.pallas_call(functools.partial(kernel, side, most), out_shape=jax.Shape...]
    all_to_all x2 -> x0, starting transfers between devices: 35.4 us -> none  [the longest x1 21.8 us: on_device(): lax.all_to_all(packed.astype(jnp.bfloat16).reshape(bank_count, slots_most...]
    dot_general x8 -> x0, matrix products: 20.1 us -> none  [the longest x1 8.41 us: on_device(): jnp.dot(flattened_rows, value_projection, preferred_element_type=jnp.floa...]
    all_to_all x2 -> x0, blocking collectives: 14.9 us -> none  [the longest x1 8.54 us: copy_for_each(): lax.all_to_all(jnp.broadcast_to(value[None], (peers, *value.shape)), axis...]
    reshape x6 -> x0, local copies, waits for them, and re-layouts: 14.3 us -> none  [the longest x1 9.85 us: on_device(): flattened_rows = images.reshape(requests_here * local_rows, images.shape[2])]
    unnamed x13 -> x1, local copies, waits for them, and re-layouts: 9.64 us -> 1.67 us
    dot_general x1 -> x0, local copies, waits for them, and re-layouts: 6.41 us -> none  [on_device(): jnp.dot(flattened_rows, key_projection, preferred_element_type=jnp.float32)]
    all_to_all x2 -> x0, waiting for transfers between devices: 4.39 us -> none  [the longest x1 4.39 us: on_device(): lax.all_to_all(raised_output, 'aa', split_axis=0, concat_axis=0, tiled=True)]
  transfers between devices with their start and end apart: 2 -> 0, of which waited for: 1 -> 0; matrix products, arithmetic and copies ran while one was open for 41% -> 0% of each run, Pallas kernels for 0% -> 0%
where the time goes in v1:
time: 60.1 us; the launch traced here: 60 us
  Pallas kernels  58.3 us (97%)
  local copies, waits for them, and re-layouts  1.67 us (3%)
    pallas_call x1, Pallas kernels, on_device(): pl.pallas_call(functools.partial(kernel, side, most), out_shape=jax.Shape...  58.3 us
    unnamed x1, local copies, waits for them, and re-layouts  1.67 us

profile of v1, /device:TPU:513, one launch (start us, length us, event | category | flops | bytes accessed | tf_op | source)
XLA Modules:
  0.0 60.0 jit_solution(10590427334156153254)
XLA Ops:
  0.0 58.3 %adapter_attention.1 = bf16[64,2048]{1,0:T(8,128)(2,1)} custom-call(bf16[768,4096]{1,0:T(8,128)(2,1)} %bitcast.10, bf16[4096,512]{1,0:T(8,128)(2,1)} %wk.1, bf16[4096,512]{1,0:T(8,128)(2,1)} %wv.1, f32[1,128]{1,0:T(1,128)} %bitcast.13, bf16[128,2048]{1,0:T(8,128)(2,1)} %hidden.1, bf16[128,1024]{1,0:T(8,128)(2,1)} %base.1, bf16[16,4096]{1,0:T(8,128)(2,1)} %bitcast.11, ...), custom_call_target="tpu_custom_call" | custom-call | tf_op jit(solution)/shard_map/adapter_attention/pallas_call | solution.py:365
  58.3 1.7 %copy.12 = bf16[64,2048]{1,0:T(8,128)(2,1)} copy(bf16[64,2048]{1,0:T(8,128)(2,1)} %adapter_attention.1) | data formatting | bytes 524288

commit v2 on v1

--- a/solution.py
+++ b/solution.py
@@ -61,6 +61,9 @@
     keys,
     values,
     bias,
+    scores,
+    weights,
+    totals,
     local_sem,
     adapter_send,
     adapter_recv,
@@ -93,7 +96,19 @@
     def along_row(k):
         return {"aa": y * side + (x + k) % side}
 
-    own_slot = parity * (group + y // 2) + (1 - parity) * (x // 2)
+    def neighbour(ring, k):
+        across = y * side + (x + k + side) % side
+        along = (y + k + side) % side * side + x
+        row_wise = 1 - parity if ring == 1 else parity
+        return {"aa": row_wise * across + (1 - row_wise) * along}
+
+    def slot_of(ring, k):
+        even = (x + k + side) % side // 2
+        odd = group + (y + k + side) % side // 2
+        row_wise = 1 - parity if ring == 1 else parity
+        return row_wise * even + (1 - row_wise) * odd
+
+    own_slot = slot_of(1, 0)
 
     barrier = pltpu.get_barrier_semaphore()
     pl.semaphore_signal(barrier, inc=1, device_id=partner, device_id_type=MESH)
@@ -106,22 +121,89 @@
     own_down = adapters.at[own_slot, :, pl.ds(0, half_model)]
     own_up = adapters.at[own_slot, :, pl.ds(half_model, half_query)]
     pairs = (
+        (down.at[:, pl.ds(model_at, half_model)], own_down),
+        (up.at[:, pl.ds(query_at, half_query)], own_up),
         (ids, ids_v),
         (hidden, hidden_v),
-        (down.at[:, pl.ds(model_at, half_model)], own_down),
-        (up.at[:, pl.ds(query_at, half_query)], own_up),
-        (used, used_v),
-        (gain, gain_v),
         (images, images_v),
         (wk, wk_v),
         (wv, wv_v),
+        (gain, gain_v),
+        (used, used_v),
         (base, base_v),
     )
     local = [pltpu.make_async_copy(s, d, local_sem.at[i]) for i, (s, d) in enumerate(pairs)]
-    for copy in local:
+    for copy in local[:4]:
         copy.start()
 
+    sends = []
+
+    def send(source, target, send_sem, recv_sem, device):
+        copy = pltpu.make_async_remote_copy(
+            src_ref=source,
+            dst_ref=target,
+            send_sem=send_sem,
+            recv_sem=recv_sem,
+            device_id=device,
+            device_id_type=MESH,
+        )
+        copy.start()
+        sends.append(copy)
+
+    def arrived(ref, send_sem, recv_sem):
+        pltpu.make_async_remote_copy(
+            src_ref=ref,
+            dst_ref=ref,
+            send_sem=send_sem,
+            recv_sem=recv_sem,
+            device_id=partner,
+            device_id_type=MESH,
+        ).wait_recv()
+
+    last = side // 2
+    turn = 1 - 2 * core
+
+    def ways(step):
+        return (1, -1) if step < last else (turn,)
+
+    def pass_on(step):
+        ring = 1 if step % 2 else 2
+        for way in ways(step):
+            at = slot_of(ring, -way * (step - 1))
+            send(
+                adapters.at[at],
+                adapters.at[at],
+                adapter_send.at[passes.pop()],
+                adapter_recv.at[at],
+                neighbour(ring, way),
+            )
+
+    def taken(step):
+        ring = 2 if step % 2 else 1
+        for way in ways(step):
+            at = slot_of(ring, -way * step)
+            arrived(adapters.at[at], adapter_send.at[0], adapter_recv.at[at])
+
+    passes = list(range(side))
+
+    def send_rows(distance):
+        for k in (distance, side - distance) if distance < last else (distance,):
+            to_y, to_x = (y + k) % side, (x + k) % side
+            send(packed.at[to_y], received.at[y], row_send.at[k], row_recv.at[y], down_column(k))
+            send(
+                packed.at[side + to_x],
+                received.at[side + x],
+                row_send.at[side + k],
+                row_recv.at[side + x],
+                along_row(k),
+            )
+
     local[0].wait()
+    local[1].wait()
+    pl.semaphore_wait(barrier, 2 * side - 1)
+    pass_on(1)
+
+    local[2].wait()
     owner = ids_v[...]
     hot = (iota((banks, requests), 0) == owner).astype(BF16)
     earlier = (iota((requests, requests), 0) < iota((requests, requests), 1)).astype(BF16)
@@ -137,80 +219,54 @@
     )
     slot = place * most + standing
     placing[...] = (iota((banks * most, requests), 0) == slot).astype(BF16)
-    local[1].wait()
+    local[3].wait()
+    for copy in local[4:]:
+        copy.start()
     packed[...] = (
         dot(placing[...], hidden_v[...]).astype(BF16).reshape(2 * side, chunk, half_model)
     )
     received[y] = packed[y]
     received[side + x] = packed[side + x]
-    local[2].wait()
-    local[3].wait()
-
-    pl.semaphore_wait(barrier, 2 * side - 1)
-
-    sends = []
-
-    def send(source, target, send_sem, recv_sem, device):
-        copy = pltpu.make_async_remote_copy(
-            src_ref=source,
-            dst_ref=target,
-            send_sem=send_sem,
-            recv_sem=recv_sem,
-            device_id=device,
-            device_id_type=MESH,
-        )
-        copy.start()
-        sends.append(copy)
-        return copy
-
-    order = sorted(range(1, side), key=lambda k: -min(k, side - k))
-    for k in order:
-        peer = parity * ((y + k) % side * side + x) + (1 - parity) * (y * side + (x + k) % side)
-        send(
-            adapters.at[own_slot],
-            adapters.at[own_slot],
-            adapter_send.at[k],
-            adapter_recv.at[own_slot],
-            {"aa": peer},
-        )
-    for k in order:
-        to_y, to_x = (y + k) % side, (x + k) % side
-        send(packed.at[to_y], received.at[y], row_send.at[k], row_recv.at[y], down_column(k))
-        send(
-            packed.at[side + to_x],
-            received.at[side + x],
-            row_send.at[side + k],
-            row_recv.at[side + x],
-            along_row(k),
-        )
+    distances = sorted(range(1, last + 1), key=lambda d: -min(d, side - d) * (1 if d < last else 0.6))
+    send_rows(distances[0])
 
     local[4].wait()
     local[5].wait()
-    local[6].wait()
     local[7].wait()
     wide = 2 * head
-
-    def project_keys(n, carry):
-        at = pl.multiple_of(n * wide, wide)
-        raw = dot(images_v[...], wk_v[:, pl.ds(at, wide)])
+    key_parts = wk.shape[1] // wide
+
+    def project_keys(n):
+        at = n * wide
+        raw = dot(images_v[...], wk_v[:, at : at + wide])
         for part in range(2):
             one = raw[:, part * head : (part + 1) * head]
             scale = lax.rsqrt(jnp.mean(one * one, axis=1, keepdims=True) + 1e-06)
-            keys[:, :, pl.ds(pl.multiple_of(at + part * head, head), head)] = (
+            keys[:, :, at + part * head : at + (part + 1) * head] = (
                 (one * scale * gain_v[...]).astype(BF16).reshape(tokens, ours, head)
             )
-        return carry
-
-    lax.fori_loop(0, wk.shape[1] // wide, project_keys, 0)
+
+    def project_values(n):
+        at = n * wide
+        raw = dot(images_v[...], wv_v[:, at : at + wide])
+        values[:, :, at : at + wide] = raw.astype(BF16).reshape(tokens, ours, wide)
+
+    for part in range(2 * key_parts):
+        if part == key_parts:
+            local[6].wait()
+        if part < key_parts:
+            project_keys(part)
+        else:
+            project_values(part - key_parts)
+        if part + 1 < last:
+            taken(part + 1)
+            pass_on(part + 2)
+            send_rows(distances[part + 1])
+    for step in range(2 * key_parts + 1, last):
+        taken(step)
+        pass_on(step + 1)
+        send_rows(distances[step])
     local[8].wait()
-
-    def project_values(n, carry):
-        at = pl.multiple_of(n * wide, wide)
-        raw = dot(images_v[...], wv_v[:, pl.ds(at, wide)])
-        values[:, :, pl.ds(at, wide)] = raw.astype(BF16).reshape(tokens, ours, wide)
-        return carry
-
-    lax.fori_loop(0, wv.shape[1] // wide, project_values, 0)
 
     lanes = tokens * BLOCK
     heads_each = (2 * half_query // head) // (wk.shape[1] // head)
@@ -228,19 +284,7 @@
         count = dot(counts, spread)[0:1]
         bias[b] = jnp.where(same & (tile.astype(F32) < count), 0.0, -1e30)
 
-    def arrived(ref, send_sem, recv_sem):
-        pltpu.make_async_remote_copy(
-            src_ref=ref,
-            dst_ref=ref,
-            send_sem=send_sem,
-            recv_sem=recv_sem,
-            device_id=partner,
-            device_id_type=MESH,
-        ).wait_recv()
-
-    for k in range(1, side):
-        other = (own_slot + k) % side
-        arrived(adapters.at[other], adapter_send.at[k], adapter_recv.at[other])
+    taken(last)
     slots = side * chunk
     in_slot = (iota((slots, group * rank), 0) & (chunk - 1)) // most
     keep = in_slot == iota((slots, group * rank), 1) // rank
@@ -256,9 +300,11 @@
             NT,
         )
         low_own[kind] = jnp.where(keep, low, 0.0)
-    send(low_own, low_other, low_send, low_recv, partner)
-    arrived(low_other, low_send, low_recv)
-    for kind in range(2):
+        send(
+            low_own.at[kind], low_other.at[kind], low_send.at[kind], low_recv.at[kind], partner
+        )
+    for kind, here in ((0, y), (1, x)):
+        arrived(low_other.at[kind], low_send.at[kind], low_recv.at[kind])
         low = (low_own[kind] + low_other[kind]).astype(BF16)
         result = dot(
             low,
@@ -269,18 +315,16 @@
         raised[kind * side : (kind + 1) * side] = result.astype(BF16).reshape(
             side, chunk, half_query
         )
-    returned[y] = raised[y]
-    returned[side + x] = raised[side + x]
-    for k in order:
-        to_y, to_x = (y + k) % side, (x + k) % side
-        send(raised.at[to_y], returned.at[y], back_send.at[k], back_recv.at[y], down_column(k))
-        send(
-            raised.at[side + to_x],
-            returned.at[side + x],
-            back_send.at[side + k],
-            back_recv.at[side + x],
-            along_row(k),
-        )
+        returned[kind * side + here] = raised[kind * side + here]
+        for distance in range(last, 0, -1):
+            for k in (distance, side - distance) if distance < last else (distance,):
+                send(
+                    raised.at[kind * side + (here + k) % side],
+                    returned.at[kind * side + here],
+                    back_send.at[kind * side + k],
+                    back_recv.at[kind * side + here],
+                    along_row(k) if kind else down_column(k),
+                )
     local[9].wait()
     for kind, here in ((0, y), (1, x)):
         for k in range(1, side):
@@ -292,31 +336,39 @@
     q_send[...] = q_own[1 - core]
     send(q_send, q_other, q_send_sem, q_recv_sem, partner)
 
+    heads_kv = half_query // head // heads_each
+    cells = [(b, g) for b in range(ours // BLOCK) for g in range(heads_kv)]
+
     def attend(q, part):
-        for b in range(ours // BLOCK):
+        first_kv = part * (heads_kv * head)
+        for n, (b, g) in enumerate(cells):
             at = slice(b * BLOCK, (b + 1) * BLOCK)
-            for g in range(half_query // head // heads_each):
-                first = part * half_query + g * heads_each * head
-                kv = pl.multiple_of(
-                    part * (half_query // heads_each) + g * head, head
-                )
-                block = jnp.concatenate(
-                    [
-                        q[at, (g * heads_each + i) * head : (g * heads_each + i + 1) * head]
-                        for i in range(heads_each)
-                    ],
-                    axis=0,
-                )
-                key = keys[:, at, pl.ds(kv, head)].reshape(lanes, head)
-                value = values[:, at, pl.ds(kv, head)].reshape(lanes, head)
-                score = dot(block, key, NT) * (1.0 / math.sqrt(head)) + bias[b]
-                weight = jnp.exp(score - jnp.max(score, axis=1, keepdims=True))
-                total = jnp.sum(weight, axis=1, keepdims=True)
-                result = (dot(weight.astype(BF16), value) / total).astype(BF16)
-                for i in range(heads_each):
-                    out[at, pl.ds(pl.multiple_of(first + i * head, head), head)] = result[
-                        i * BLOCK : (i + 1) * BLOCK
-                    ]
+            block = jnp.concatenate(
+                [
+                    q[at, (g * heads_each + i) * head : (g * heads_each + i + 1) * head]
+                    for i in range(heads_each)
+                ],
+                axis=0,
+            )
+            key = keys[:, at, pl.ds(pl.multiple_of(first_kv + g * head, head), head)]
+            scores[n] = (
+                dot(block, key.reshape(lanes, head), NT) * (1.0 / math.sqrt(head)) + bias[b]
+            )
+        peaks = jnp.max(scores[...], axis=2, keepdims=True)
+        weight = jnp.exp(scores[...] - peaks)
+        totals[...] = jnp.broadcast_to(
+            jnp.sum(weight, axis=2, keepdims=True), totals.shape
+        )
+        weights[...] = weight.astype(BF16)
+        for n, (b, g) in enumerate(cells):
+            at = slice(b * BLOCK, (b + 1) * BLOCK)
+            value = values[:, at, pl.ds(pl.multiple_of(first_kv + g * head, head), head)]
+            result = (dot(weights[n], value.reshape(lanes, head)) / totals[n]).astype(BF16)
+            for i in range(heads_each):
+                column = part * half_query + (g * heads_each + i) * head
+                out[at, pl.ds(pl.multiple_of(column, head), head)] = result[
+                    i * BLOCK : (i + 1) * BLOCK
+                ]
 
     attend(q_own[core], core)
     arrived(q_other, q_send_sem, q_recv_sem)
@@ -349,6 +401,7 @@
     chunk = group * most
     rank = adapter_up_matrix.shape[1]
     heads_each = 2 * half_query // kvw
+    cells = ours // BLOCK * (half_query // head // heads_each)
     args = (
         jnp.transpose(images, (1, 0, 2)).reshape(tokens * ours, model),
         key_projection,
@@ -390,6 +443,9 @@
             pltpu.VMEM((tokens, ours, kvw), BF16),
             pltpu.VMEM((tokens, ours, kvw), BF16),
             pltpu.VMEM((ours // BLOCK, heads_each * BLOCK, tokens * BLOCK), F32),
+            pltpu.VMEM((cells, heads_each * BLOCK, tokens * BLOCK), F32),
+            pltpu.VMEM((cells, heads_each * BLOCK, tokens * BLOCK), BF16),
+            pltpu.VMEM((cells, heads_each * BLOCK, head), F32),
             dma((10,)),
             dma((side,)),
             dma((side,)),
@@ -397,8 +453,8 @@
             dma((2 * side,)),
             dma((2 * side,)),
             dma((2 * side,)),
-            dma(()),
-            dma(()),
+            dma((2,)),
+            dma((2,)),
             dma(()),
             dma(()),
         ],

time: 60.1 us -> 61.4 us (1.022)
  Pallas kernels: 58.3 us -> 59.6 us
    pallas_call x1, Pallas kernels: 58.3 us -> 59.6 us  [on_device(): pl.pallas_call(functools.partial(kernel, side, most), out_shape=jax.Shape...]
where the time goes in v2:
time: 61.4 us; the launch traced here: 61.3 us
  Pallas kernels  59.6 us (97%)
  local copies, waits for them, and re-layouts  1.67 us (3%)
    pallas_call x1, Pallas kernels, on_device(): pl.pallas_call(functools.partial(kernel, side, most), out_shape=jax.Shape...  59.6 us
    unnamed x1, local copies, waits for them, and re-layouts  1.67 us

profile of v2, /device:TPU:513, one launch (start us, length us, event | category | flops | bytes accessed | tf_op | source)
XLA Modules:
  0.0 61.3 jit_solution(11311603803447471766)
XLA Ops:
  0.0 59.6 %adapter_attention.1 = bf16[64,2048]{1,0:T(8,128)(2,1)} custom-call(bf16[768,4096]{1,0:T(8,128)(2,1)} %bitcast.10, bf16[4096,512]{1,0:T(8,128)(2,1)} %wk.1, bf16[4096,512]{1,0:T(8,128)(2,1)} %wv.1, f32[1,128]{1,0:T(1,128)} %bitcast.13, bf16[128,2048]{1,0:T(8,128)(2,1)} %hidden.1, bf16[128,1024]{1,0:T(8,128)(2,1)} %base.1, bf16[16,4096]{1,0:T(8,128)(2,1)} %bitcast.11, ...), custom_call_target="tpu_custom_call" | custom-call | tf_op jit(solution)/shard_map/adapter_attention/pallas_call | solution.py:418
  59.6 1.7 %copy.12 = bf16[64,2048]{1,0:T(8,128)(2,1)} copy(bf16[64,2048]{1,0:T(8,128)(2,1)} %adapter_attention.1) | data formatting | bytes 524288

commit v3 on v2

--- a/solution.py
+++ b/solution.py
@@ -64,6 +64,7 @@
     scores,
     weights,
     totals,
+    gate,
     local_sem,
     adapter_send,
     adapter_recv,
@@ -90,31 +91,36 @@
     tokens, ours = keys.shape[0], keys.shape[1]
     head = gain.shape[1]
 
-    def down_column(k):
-        return {"aa": ((y + k) % side) * side + x}
-
-    def along_row(k):
-        return {"aa": y * side + (x + k) % side}
-
-    def neighbour(ring, k):
-        across = y * side + (x + k + side) % side
-        along = (y + k + side) % side * side + x
-        row_wise = 1 - parity if ring == 1 else parity
-        return {"aa": row_wise * across + (1 - row_wise) * along}
-
-    def slot_of(ring, k):
-        even = (x + k + side) % side // 2
-        odd = group + (y + k + side) % side // 2
-        row_wise = 1 - parity if ring == 1 else parity
-        return row_wise * even + (1 - row_wise) * odd
-
-    own_slot = slot_of(1, 0)
+    own_slot = (1 - parity) * (x // 2) + parity * (group + y // 2)
+
+    def rank_of(index):
+        return (index + banks - 1 + core) % banks
+
+    mine = rank_of(me)
+    last_column = jnp.where((core == 0) & (x == 0), 1, 0)
+    last_row = jnp.where((core == 0) & (y == 0), 1, 0)
+    around = [
+        (index, gate_at, own_gate)
+        for k in range(1, side)
+        for index, gate_at, own_gate in (
+            ((y + k) % side * side + x, (y + k) % side, y),
+            (y * side + (x + k) % side, side + (x + k) % side, side + x),
+        )
+    ]
 
     barrier = pltpu.get_barrier_semaphore()
-    pl.semaphore_signal(barrier, inc=1, device_id=partner, device_id_type=MESH)
-    for k in range(1, side):
-        pl.semaphore_signal(barrier, inc=1, device_id=down_column(k), device_id_type=MESH)
-        pl.semaphore_signal(barrier, inc=1, device_id=along_row(k), device_id_type=MESH)
+    pl.semaphore_signal(barrier, inc=1, device_id={"aa": me}, device_id_type=MESH)
+    earlier_peers = 2 - core
+    for index, gate_at, own_gate in around:
+        earlier_peers = earlier_peers + jnp.where(rank_of(index) < mine, 1, 0)
+
+        @pl.when(rank_of(index) > mine)
+        def _(index=index):
+            pl.semaphore_signal(barrier, inc=1, device_id={"aa": index}, device_id_type=MESH)
+
+    @pl.when(core == 1)
+    def _():
+        pl.semaphore_signal(barrier, inc=1, device_id=partner, device_id_type=MESH)
 
     model_at = pl.multiple_of(core * half_model, half_model)
     query_at = pl.multiple_of(core * half_query, half_query)
@@ -136,19 +142,25 @@
     for copy in local[:4]:
         copy.start()
 
-    sends = []
-
-    def send(source, target, send_sem, recv_sem, device):
-        copy = pltpu.make_async_remote_copy(
+    def start(source, target, send_sem, recv_sem, device):
+        pltpu.make_async_remote_copy(
             src_ref=source,
             dst_ref=target,
             send_sem=send_sem,
             recv_sem=recv_sem,
             device_id=device,
             device_id_type=MESH,
-        )
-        copy.start()
-        sends.append(copy)
+        ).start()
+
+    def left(ref, send_sem, recv_sem):
+        pltpu.make_async_remote_copy(
+            src_ref=ref,
+            dst_ref=ref,
+            send_sem=send_sem,
+            recv_sem=recv_sem,
+            device_id=partner,
+            device_id_type=MESH,
+        ).wait_send()
 
     def arrived(ref, send_sem, recv_sem):
         pltpu.make_async_remote_copy(
@@ -160,48 +172,82 @@
             device_id_type=MESH,
         ).wait_recv()
 
-    last = side // 2
-    turn = 1 - 2 * core
-
-    def ways(step):
-        return (1, -1) if step < last else (turn,)
-
-    def pass_on(step):
-        ring = 1 if step % 2 else 2
-        for way in ways(step):
-            at = slot_of(ring, -way * (step - 1))
-            send(
-                adapters.at[at],
-                adapters.at[at],
-                adapter_send.at[passes.pop()],
-                adapter_recv.at[at],
-                neighbour(ring, way),
+    def to_row(p, adapter, rows):
+        at = (p + last_row) % side
+        index = y * side + at
+
+        @pl.when(at != x)
+        def _():
+            if adapter:
+
+                @pl.when(rank_of(index) > mine)
+                def _():
+                    pl.semaphore_wait(gate.at[side + at], 1)
+
+                @pl.when(parity == 0)
+                def _():
+                    start(
+                        adapters.at[own_slot],
+                        adapters.at[own_slot],
+                        adapter_send.at[at],
+                        adapter_recv.at[own_slot],
+                        {"aa": index},
+                    )
+
+            if rows:
+                start(
+                    packed.at[side + at],
+                    received.at[side + x],
+                    row_send.at[side + at],
+                    row_recv.at[side + x],
+                    {"aa": index},
+                )
+
+    def to_column(p):
+        at = (p + last_column) % side
+        index = at * side + x
+
+        @pl.when(at != y)
+        def _():
+            @pl.when(rank_of(index) > mine)
+            def _():
+                pl.semaphore_wait(gate.at[at], 1)
+
+            @pl.when(parity == 1)
+            def _():
+                start(
+                    adapters.at[own_slot],
+                    adapters.at[own_slot],
+                    adapter_send.at[at],
+                    adapter_recv.at[own_slot],
+                    {"aa": index},
+                )
+
+            start(
+                packed.at[at],
+                received.at[y],
+                row_send.at[at],
+                row_recv.at[y],
+                {"aa": index},
             )
 
-    def taken(step):
-        ring = 2 if step % 2 else 1
-        for way in ways(step):
-            at = slot_of(ring, -way * step)
-            arrived(adapters.at[at], adapter_send.at[0], adapter_recv.at[at])
-
-    passes = list(range(side))
-
-    def send_rows(distance):
-        for k in (distance, side - distance) if distance < last else (distance,):
-            to_y, to_x = (y + k) % side, (x + k) % side
-            send(packed.at[to_y], received.at[y], row_send.at[k], row_recv.at[y], down_column(k))
-            send(
-                packed.at[side + to_x],
-                received.at[side + x],
-                row_send.at[side + k],
-                row_recv.at[side + x],
-                along_row(k),
+    pl.semaphore_wait(barrier, earlier_peers)
+    for index, gate_at, own_gate in around:
+
+        @pl.when(rank_of(index) < mine)
+        def _(index=index, own_gate=own_gate):
+            pl.semaphore_signal(
+                gate.at[own_gate], inc=1, device_id={"aa": index}, device_id_type=MESH
             )
+
+    @pl.when(core == 0)
+    def _():
+        pl.semaphore_signal(gate.at[2 * side], inc=1, device_id=partner, device_id_type=MESH)
 
     local[0].wait()
     local[1].wait()
-    pl.semaphore_wait(barrier, 2 * side - 1)
-    pass_on(1)
+    for p in range(side - 1):
+        to_row(p, True, False)
 
     local[2].wait()
     owner = ids_v[...]
@@ -227,8 +273,12 @@
     )
     received[y] = packed[y]
     received[side + x] = packed[side + x]
-    distances = sorted(range(1, last + 1), key=lambda d: -min(d, side - d) * (1 if d < last else 0.6))
-    send_rows(distances[0])
+    for p in range(side - 1):
+        to_row(p, False, True)
+    for p in range(side - 1):
+        to_column(p)
+    to_row(side - 1, True, True)
+    to_column(side - 1)
 
     local[4].wait()
     local[5].wait()
@@ -258,14 +308,6 @@
             project_keys(part)
         else:
             project_values(part - key_parts)
-        if part + 1 < last:
-            taken(part + 1)
-            pass_on(part + 2)
-            send_rows(distances[part + 1])
-    for step in range(2 * key_parts + 1, last):
-        taken(step)
-        pass_on(step + 1)
-        send_rows(distances[step])
     local[8].wait()
 
     lanes = tokens * BLOCK
@@ -284,14 +326,20 @@
         count = dot(counts, spread)[0:1]
         bias[b] = jnp.where(same & (tile.astype(F32) < count), 0.0, -1e30)
 
-    taken(last)
     slots = side * chunk
     in_slot = (iota((slots, group * rank), 0) & (chunk - 1)) // most
     keep = in_slot == iota((slots, group * rank), 1) // rank
+
     for kind, here in ((0, y), (1, x)):
+        for slot_at in range(kind * group, (kind + 1) * group):
+
+            @pl.when(own_slot != slot_at)
+            def _(slot_at=slot_at):
+                arrived(adapters.at[slot_at], adapter_send.at[0], adapter_recv.at[slot_at])
+
         for k in range(1, side):
             source = kind * side + (here + k) % side
-            arrived(received.at[source], row_send.at[k], row_recv.at[source])
+            arrived(received.at[source], row_send.at[source], row_recv.at[source])
         low = dot(
             received[kind * side : (kind + 1) * side].reshape(slots, half_model),
             adapters[kind * group : (kind + 1) * group, :, :half_model].reshape(
@@ -300,10 +348,13 @@
             NT,
         )
         low_own[kind] = jnp.where(keep, low, 0.0)
-        send(
-            low_own.at[kind], low_other.at[kind], low_send.at[kind], low_recv.at[kind], partner
-        )
-    for kind, here in ((0, y), (1, x)):
+        if kind == 0:
+
+            @pl.when(core == 1)
+            def _():
+                pl.semaphore_wait(gate.at[2 * side], 1)
+
+        start(low_own.at[kind], low_other.at[kind], low_send.at[kind], low_recv.at[kind], partner)
         arrived(low_other.at[kind], low_send.at[kind], low_recv.at[kind])
         low = (low_own[kind] + low_other[kind]).astype(BF16)
         result = dot(
@@ -316,14 +367,15 @@
             side, chunk, half_query
         )
         returned[kind * side + here] = raised[kind * side + here]
-        for distance in range(last, 0, -1):
-            for k in (distance, side - distance) if distance < last else (distance,):
-                send(
-                    raised.at[kind * side + (here + k) % side],
+        for distance in range(side // 2, 0, -1):
+            for k in (distance, side - distance) if 2 * distance < side else (distance,):
+                to = (here + k) % side
+                start(
+                    raised.at[kind * side + to],
                     returned.at[kind * side + here],
-                    back_send.at[kind * side + k],
+                    back_send.at[kind * side + to],
                     back_recv.at[kind * side + here],
-                    along_row(k) if kind else down_column(k),
+                    {"aa": y * side + to} if kind else {"aa": to * side + x},
                 )
     local[9].wait()
     for kind, here in ((0, y), (1, x)):
@@ -334,7 +386,7 @@
     query = (base_v[...].astype(F32) + delta).astype(BF16)
     q_own[...] = query.reshape(2, ours, half_query)
     q_send[...] = q_own[1 - core]
-    send(q_send, q_other, q_send_sem, q_recv_sem, partner)
+    start(q_send, q_other, q_send_sem, q_recv_sem, partner)
 
     heads_kv = half_query // head // heads_each
     cells = [(b, g) for b in range(ours // BLOCK) for g in range(heads_kv)]
@@ -373,8 +425,16 @@
     attend(q_own[core], core)
     arrived(q_other, q_send_sem, q_recv_sem)
     attend(q_other[...], 1 - core)
-    for copy in sends:
-        copy.wait_send()
+    own_at = (1 - parity) * x + parity * y
+    for k in range(1, side):
+        left(adapters.at[own_slot], adapter_send.at[(own_at + k) % side], adapter_recv.at[0])
+    for kind, here in ((0, y), (1, x)):
+        for k in range(1, side):
+            at = kind * side + (here + k) % side
+            left(packed.at[at], row_send.at[at], row_recv.at[at])
+            left(raised.at[at], back_send.at[at], back_recv.at[at])
+        left(low_own.at[kind], low_send.at[kind], low_recv.at[kind])
+    left(q_send, q_send_sem, q_recv_sem)
 
 
 def on_device(
@@ -446,6 +506,7 @@
             pltpu.VMEM((cells, heads_each * BLOCK, tokens * BLOCK), F32),
             pltpu.VMEM((cells, heads_each * BLOCK, tokens * BLOCK), BF16),
             pltpu.VMEM((cells, heads_each * BLOCK, head), F32),
+            pltpu.SemaphoreType.REGULAR((2 * side + 1,)),
             dma((10,)),
             dma((side,)),
             dma((side,)),

time: 61.4 us -> 55.9 us (0.910)
  Pallas kernels: 59.6 us -> 54 us
    pallas_call x1, Pallas kernels: 59.6 us -> 54 us  [on_device(): pl.pallas_call(functools.partial(kernel, side, most), out_shape=jax.Shape...]
where the time goes in v3:
time: 55.9 us; the launch traced here: 55.7 us
  Pallas kernels  54 us (97%)
  local copies, waits for them, and re-layouts  1.67 us (3%)
    pallas_call x1, Pallas kernels, on_device(): pl.pallas_call(functools.partial(kernel, side, most), out_shape=jax.Shape...  54 us
    unnamed x1, local copies, waits for them, and re-layouts  1.67 us

profile of v3, /device:TPU:513, one launch (start us, length us, event | category | flops | bytes accessed | tf_op | source)
XLA Modules:
  0.0 55.7 jit_solution(3077236726648819254)
XLA Ops:
  0.0 54.0 %adapter_attention.1 = bf16[64,2048]{1,0:T(8,128)(2,1)} custom-call(bf16[768,4096]{1,0:T(8,128)(2,1)} %bitcast.10, bf16[4096,512]{1,0:T(8,128)(2,1)} %wk.1, bf16[4096,512]{1,0:T(8,128)(2,1)} %wv.1, f32[1,128]{1,0:T(1,128)} %bitcast.13, bf16[128,2048]{1,0:T(8,128)(2,1)} %hidden.1, bf16[128,1024]{1,0:T(8,128)(2,1)} %base.1, bf16[16,4096]{1,0:T(8,128)(2,1)} %bitcast.11, ...), custom_call_target="tpu_custom_call" | custom-call | tf_op jit(solution)/shard_map/adapter_attention/pallas_call | solution.py:478
  54.0 1.7 %copy.12 = bf16[64,2048]{1,0:T(8,128)(2,1)} copy(bf16[64,2048]{1,0:T(8,128)(2,1)} %adapter_attention.1) | data formatting | bytes 524288

commit v4 on v3

--- a/solution.py
+++ b/solution.py
@@ -301,13 +301,8 @@
         raw = dot(images_v[...], wv_v[:, at : at + wide])
         values[:, :, at : at + wide] = raw.astype(BF16).reshape(tokens, ours, wide)
 
-    for part in range(2 * key_parts):
-        if part == key_parts:
-            local[6].wait()
-        if part < key_parts:
-            project_keys(part)
-        else:
-            project_values(part - key_parts)
+    for part in range(key_parts):
+        project_keys(part)
     local[8].wait()
 
     lanes = tokens * BLOCK
@@ -377,6 +372,9 @@
                     back_recv.at[kind * side + here],
                     {"aa": y * side + to} if kind else {"aa": to * side + x},
                 )
+    local[6].wait()
+    for part in range(key_parts):
+        project_values(part)
     local[9].wait()
     for kind, here in ((0, y), (1, x)):
         for k in range(1, side):
@@ -477,7 +475,7 @@
     dma = pltpu.SemaphoreType.DMA
     return pl.pallas_call(
         functools.partial(kernel, side, most),
-        out_shape=jax.ShapeDtypeStruct((ours, 2 * half_query), BF16),
+        out_shape=pltpu.VMEM((ours, 2 * half_query), BF16),
         in_specs=[pl.BlockSpec(memory_space=pl.ANY)] * len(args),
         out_specs=pl.BlockSpec(memory_space=pltpu.VMEM),
         scratch_shapes=[

time: 55.9 us -> 54.2 us (0.970)
  local copies, waits for them, and re-layouts: 1.67 us -> 0.71 us
  Pallas kernels: 54 us -> 53.3 us
    unnamed x1, local copies, waits for them, and re-layouts: 1.67 us -> 0.71 us
    pallas_call x1, Pallas kernels: 54 us -> 53.3 us  [on_device(): pl.pallas_call(functools.partial(kernel, side, most), out_shape=pltpu.VME...]
where the time goes in v4:
time: 54.2 us; the launch traced here: 54.1 us
  Pallas kernels  53.3 us (98%)
  local copies, waits for them, and re-layouts  0.71 us (1%)
    pallas_call x1, Pallas kernels, on_device(): pl.pallas_call(functools.partial(kernel, side, most), out_shape=pltpu.VME...  53.3 us

profile of v4, /device:TPU:513, one launch (start us, length us, event | category | flops | bytes accessed | tf_op | source)
XLA Modules:
  0.0 54.1 jit_solution(12630205512751490260)
XLA Ops:
  0.0 53.3 %adapter_attention.1 = bf16[64,2048]{1,0:T(8,128)(2,1)S(1)} custom-call(bf16[768,4096]{1,0:T(8,128)(2,1)} %bitcast.10, bf16[4096,512]{1,0:T(8,128)(2,1)} %wk.1, bf16[4096,512]{1,0:T(8,128)(2,1)} %wv.1, f32[1,128]{1,0:T(1,128)} %bitcast.13, bf16[128,2048]{1,0:T(8,128)(2,1)} %hidden.1, bf16[128,1024]{1,0:T(8,128)(2,1)} %base.1, bf16[16,4096]{1,0:T(8,128)(2,1)} %bitcast.11, ...), custom_call_target="tpu_custom_call" | custom-call | tf_op jit(solution)/shard_map/adapter_attention/pallas_call | solution.py:476
  53.4 0.7 %copy.12 = bf16[64,2048]{1,0:T(8,128)(2,1)} copy(bf16[64,2048]{1,0:T(8,128)(2,1)S(1)} %adapter_attention.1) | data formatting | bytes 524288
